TPU v7x, 32 devices: a whole 2x2x4 slice. The times are simulated.
32 devices in a mesh: rep: 2 (over x), shard: 16 (over z, y, core).
Axes of the slice: x: 2, y: 2, z: 4, core: 2. Of those that a mesh axis runs over, the one named last changes fastest.
Arguments:
- tokens_x: bfloat16 [8192, 4096], P(('rep', 'shard')), may hold values from -6 to 6
- key_grad: bfloat16 [8192, 1024], P(('rep', 'shard')), may hold values from -0.06591797 to 0.06591797
- left_root: bfloat16 [64, 512, 512], P('shard'), may hold values from -1 to 3
- slot_grads: bfloat16 [64, 512, 512], P('shard'), may hold values from -6 to 6
- right_root: bfloat16 [64, 512, 512], P('shard'), may hold values from -1 to 3
- block_slot: int32 [32], replicated, may hold values from 0 to 63, as said below
Outputs:
- grad_key: float32 [4096, 1024], P('shard')
- update: bfloat16 [512, 32, 512], P('shard')
Inputs may be any that keep to these rules, and one draw needn't show every extreme that they name: `block_slot`: the entries are distinct; slot v is slot v % 4 of shard index v // 4; no shard index holds more than 4 blocks, and some shard index holds exactly 4.
All inputs are finite; a program needn't handle non-finite values.
Results may differ from a plain program's by a relative error of at most 0.006.
Values may be sent and summed in bfloat16 or wider, within the bound.
A program may use at most 128 MiB of HBM per device.

v0:
```python
import jax
import jax.numpy as jnp
from jax import lax
from jax.sharding import PartitionSpec as P


def column_term(features, cotangent):
    return lax.dot_general(
        features, cotangent, (((0,), (0,)), ((), ())), preferred_element_type=jnp.float32
    )


def precondition(left_block, grad_block, right_block):
    left_part = jnp.einsum(
        "sij,sjk->sik", left_block, grad_block, preferred_element_type=jnp.float32
    ).astype(jnp.bfloat16)
    return jnp.einsum(
        "sij,sjk->isk", left_part, right_block, preferred_element_type=jnp.float32
    ).astype(jnp.bfloat16)


def shards(tokens_x, key_grad, left_root, slot_grads, right_root, block_slot):
    n_shard = lax.axis_size("shard")
    n_rep = lax.axis_size("rep")
    own_rows = lax.psum_scatter(
        column_term(tokens_x, key_grad), "shard", scatter_dimension=0, tiled=True
    )
    grad_key = lax.psum(own_rows, "rep")
    slot_count = left_root.shape[0]
    half_slots = slot_count // n_rep
    first_slot = lax.axis_index("rep") * half_slots

    def own_half(values):
        return lax.dynamic_slice_in_dim(values, first_slot, half_slots, 0)

    product = precondition(own_half(left_root), own_half(slot_grads), own_half(right_root))
    received = lax.all_to_all(product, "shard", split_axis=0, concat_axis=1, tiled=True)
    joined = lax.all_gather(received, "rep", axis=1, tiled=True)
    owner = block_slot // slot_count
    within = block_slot % slot_count
    position = (
        within // half_slots * (n_shard * half_slots) + owner * half_slots + within % half_slots
    )
    update = jnp.take(joined, position, axis=1)
    return (grad_key, update)


def solution(mesh):
    return jax.shard_map(
        shards,
        mesh=mesh,
        in_specs=(
            P(("rep", "shard"), None),
            P(("rep", "shard"), None),
            P("shard", None, None),
            P("shard", None, None),
            P("shard", None, None),
            P(),
        ),
        out_specs=(P("shard", None), P("shard", None, None)),
        check_vma=False,
    )
```

profile of v0, /device:TPU:0, one launch (start us, length us, event | category | flops | bytes accessed | tf_op | source)
XLA Modules:
  0.0 247.9 jit_solution(18152596970215478150)
XLA Ops:
  8.0 0.0 copy-start
  8.0 0.0 reduce-scatter.2.cloned.1.call-start
  8.1 1.5 copy-done
  9.6 9.2 %fusion.9 = f32[4096,1024]{1,0:T(8,128)} fusion(bf16[256,4096]{1,0:T(8,128)(2,1)S(1)} %copy-done, bf16[256,1024]{1,0:T(8,128)(2,1)} %param.7), kind=kOutput, calls=%fused_computation.23 | convolution fusion | flops 2147483648 | bytes 19398656 | tf_op jit(solution)/shard_map/dot_general | solution.py:8
  18.8 0.0 reduce-scatter.2.cloned.1.call-update
  18.8 0.0 all-gather.2.cloned.1.call-start
  18.8 4.1 %fusion = bf16[512,2,512]{0,2,1:T(8,128)(2,1)} fusion(bf16[4,512,512]{2,1,0:T(8,128)(2,1)} %param.9, s32[]{:T(128)S(6)} %select_n.37, bf16[4,512,512]{2,1,0:T(8,128)(2,1)} %param.8, bf16[4,512,512]{2,1,0:T(8,128)(2,1)} %param.10), kind=kOutput, calls=%fused_computation.3 | convolution fusion | flops 1074790400 | bytes 4195840 | tf_op jit(solution)/shard_map/sij,sjk->isk/dot_general | solution.py:17
  22.9 2.5 %copy.14 = bf16[512,2,512]{2,1,0:T(2,128)(2,1)S(1)} copy(bf16[512,2,512]{0,2,1:T(8,128)(2,1)} %fusion) | data formatting | bytes 2097152 | tf_op jit(solution)/shard_map/convert_element_type | solution.py:19
  25.4 31.9 %all_to_all.18 = bf16[512,2,512]{2,1,0:T(2,128)(2,1)S(1)} all-to-all(bf16[512,2,512]{2,1,0:T(2,128)(2,1)S(1)} %copy.14), channel_id=1, replica_groups=mesh['rep'=2,'shard'=16] {'shard'}, dimensions={0} | all-to-all | bytes 2097152 | tf_op jit(solution)/shard_map/all_to_all | solution.py:37
  57.3 0.2 copy.15
  57.5 0.0 copy-start.1
  57.5 1.0 copy.16
  58.6 0.0 all-gather.2.cloned.1.call-update
  58.6 0.0 all-reduce.2.cloned.1.call-start
  58.6 140.4 %reduce-scatter.2.cloned.1.call-done = f32[256,1024]{1,0:T(8,128)} async-done(((f32[4096,1024]{1,0:T(8,128)}), f32[256,1024]{1,0:T(8,128)}) %reduce-scatter.2.cloned.1.call-update) | async-done | bytes 1048592 | tf_op jit(solution)/shard_map/reduce_scatter | solution.py:25
  199.0 0.0 all-reduce.2.cloned.1.call-update
  199.0 0.0 copy-done.1
  199.1 0.0 all-gather.2.cloned.1.call-done
  199.1 2.2 gather_fusion
  201.3 0.2 select_bitcast_fusion
  201.5 1.5 copy.17
  203.0 35.1 %all-reduce.2.cloned.1.call-done = f32[256,1024]{1,0:T(8,128)} async-done(((f32[256,1024]{1,0:T(8,128)}), f32[256,1024]{1,0:T(8,128)}) %all-reduce.2.cloned.1.call-update) | async-done | bytes 1048592 | tf_op jit(solution)/shard_map/psum | solution.py:28
  238.2 2.3 copy.20
  (2 shorter events, 0.0 us)
Async XLA Ops:
  8.0 1.6 copy-start
  8.0 191.0 %reduce-scatter.2.cloned.1.call-start = ((), (), s32[]{:S(2)}) async-start(), calls=%async_computation.2 | async-start | bytes 17825792 | tf_op jit(solution)/shard_map/reduce_scatter | solution.py:25
  18.8 180.3 %all-gather.2.cloned.1.call-start = ((), (), s32[]{:S(2)}) async-start(), calls=%async_computation.4 | async-start | bytes 3145728 | tf_op jit(solution)/shard_map/all_gather | solution.py:38
  57.5 141.5 %copy-start.1 = (s32[32]{0:T(128)S(1)}, s32[32]{0:T(128)}, u32[]{:S(2)}) copy-start(s32[32]{0:T(128)} %param.11) | copy-start | bytes 388
  58.6 179.6 %all-reduce.2.cloned.1.call-start = ((), (), s32[]{:S(2)}) async-start(), calls=%async_computation.3 | async-start | bytes 2097152 | tf_op jit(solution)/shard_map/psum | solution.py:28
Sparse Core Ops, SparseCore 0:
  18.9 180.0 reduce-scatter.1
Sparse Core Ops, SparseCore 1:
  58.7 33.3 all-gather.1
  199.1 39.0 all-reduce.1
where the time goes:
time: 248 us
  waiting for transfers between devices  176 us (71%)
  blocking collectives  31.9 us (13%)
  between operations  15.6 us (6%)
  matrix products  13.3 us (5%)
  local copies, waits for them, and re-layouts  11.3 us (5%)
    reduce_scatter x1, waiting for transfers between devices, shards(): lax.psum_scatter(column_term(tokens_x, key_grad), 'shard', scatter_dimens...  140 us
    psum x1, waiting for transfers between devices, shards(): grad_key = lax.psum(own_rows, 'rep')  35.1 us
    all_to_all x1, blocking collectives, shards(): lax.all_to_all(product, 'shard', split_axis=0, concat_axis=1, tiled=True)  31.9 us
    dot_general x1, matrix products, column_term(): lax.dot_general(features, cotangent, (((0,), (0,)), ((), ())), preferred_...  9.16 us
    unnamed x6, local copies, waits for them, and re-layouts  5.4 us
  transfers between devices with their start and end apart: 3, of which 2 were waited for; matrix products, arithmetic and copies ran while one was open for 5% of the time, Pallas kernels for 0%

commit v1 on v0

--- a/solution.py
+++ b/solution.py
@@ -34,7 +34,9 @@
         return lax.dynamic_slice_in_dim(values, first_slot, half_slots, 0)
 
     product = precondition(own_half(left_root), own_half(slot_grads), own_half(right_root))
-    received = lax.all_to_all(product, "shard", split_axis=0, concat_axis=1, tiled=True)
+    cells = jnp.split(product, lax.axis_size("shard"), axis=0)
+    got = lax.all_to_all(jnp.stack(cells), "shard", 0, 0)
+    received = jnp.concatenate(got, axis=1)
     joined = lax.all_gather(received, "rep", axis=1, tiled=True)
     owner = block_slot // slot_count
     within = block_slot % slot_count

time: 248 us -> 248 us (level)
  waiting for transfers between devices: 176 us -> 180 us
  local copies, waits for them, and re-layouts: 11.3 us -> 7.72 us
    reduce_scatter x1, waiting for transfers between devices: 140 us -> 145 us  [shards(): lax.psum_scatter(column_term(tokens_x, key_grad), 'shard', scatter_dimens...]
    convert_element_type x1 -> x0, local copies, waits for them, and re-layouts: 2.5 us -> none  [precondition(): return jnp.einsum('sij,sjk->isk', left_part, right_block, preferred_eleme...]
    unnamed x6 -> x21, local copies, waits for them, and re-layouts: 5.4 us -> 5.51 us
  transfers between devices with their start and end apart: 3 -> 3, of which waited for: 2 -> 2; matrix products, arithmetic and copies ran while one was open for 5% -> 3% of each run, Pallas kernels for 0% -> 0%
where the time goes in v1:
time: 248 us
  waiting for transfers between devices  180 us (73%)
  blocking collectives  32 us (13%)
  between operations  15.7 us (6%)
  matrix products  12.3 us (5%)
  local copies, waits for them, and re-layouts  7.72 us (3%)
    reduce_scatter x1, waiting for transfers between devices, shards(): lax.psum_scatter(column_term(tokens_x, key_grad), 'shard', scatter_dimens...  145 us
    psum x1, waiting for transfers between devices, shards(): grad_key = lax.psum(own_rows, 'rep')  35.1 us
    all_to_all x1, blocking collectives, shards(): got = lax.all_to_all(jnp.stack(cells), 'shard', 0, 0)  32 us
    dot_general x1, matrix products, column_term(): lax.dot_general(features, cotangent, (((0,), (0,)), ((), ())), preferred_...  9.16 us
    unnamed x21, local copies, waits for them, and re-layouts  5.51 us
  transfers between devices with their start and end apart: 3, of which 2 were waited for; matrix products, arithmetic and copies ran while one was open for 3% of the time, Pallas kernels for 0%

profile of v1, /device:TPU:0, one launch (start us, length us, event | category | flops | bytes accessed | tf_op | source)
XLA Modules:
  0.0 247.9 jit_solution(13406744691568452154)
XLA Ops:
  8.0 0.0 copy-start
  8.0 0.0 reduce-scatter.2.cloned.1.call-start
  8.1 1.5 copy-done
  9.6 9.2 %fusion.25 = f32[4096,1024]{1,0:T(8,128)} fusion(bf16[256,4096]{1,0:T(8,128)(2,1)S(1)} %copy-done, bf16[256,1024]{1,0:T(8,128)(2,1)} %param.7), kind=kOutput, calls=%fused_computation.55 | convolution fusion | flops 2147483648 | bytes 19398656 | tf_op jit(solution)/shard_map/dot_general | solution.py:8
  18.8 0.0 reduce-scatter.2.cloned.1.call-update
  18.8 0.0 all-gather.2.cloned.1.call-start
  18.8 3.1 %fusion = bf16[512,2,512]{2,0,1:T(8,128)(2,1)S(1)} fusion(bf16[4,512,512]{2,1,0:T(8,128)(2,1)} %param.9, s32[]{:T(128)S(6)} %select_n.37, bf16[4,512,512]{2,1,0:T(8,128)(2,1)} %param.8, bf16[4,512,512]{2,1,0:T(8,128)(2,1)} %param.10), kind=kOutput, calls=%fused_computation.3 | convolution fusion | flops 1074790400 | bytes 4195840 | tf_op jit(solution)/shard_map/sij,sjk->isk/dot_general | solution.py:17
  22.2 0.0 copy-start.1
  22.2 32.0 %all_to_all.5 = bf16[16,32,2,512]{3,1,2,0:T(8,128)(2,1)} all-to-all(bf16[16,32,2,512]{3,1,2,0:T(8,128)(2,1)S(1)} %fusion.6), channel_id=1, replica_groups=mesh['rep'=2,'shard'=16] {'shard'}, dimensions={0} | all-to-all | bytes 2097152 | tf_op jit(solution)/shard_map/all_to_all | solution.py:38
  54.2 0.0 all-gather.2.cloned.1.call-update
  54.2 0.0 all-reduce.2.cloned.1.call-start
  54.3 144.7 %reduce-scatter.2.cloned.1.call-done = f32[256,1024]{1,0:T(8,128)} async-done(((f32[4096,1024]{1,0:T(8,128)}), f32[256,1024]{1,0:T(8,128)}) %reduce-scatter.2.cloned.1.call-update) | async-done | bytes 1048592 | tf_op jit(solution)/shard_map/reduce_scatter | solution.py:25
  199.0 0.0 all-reduce.2.cloned.1.call-update
  199.0 0.0 copy-done.1
  199.1 0.0 all-gather.2.cloned.1.call-done
  199.1 2.2 gather_fusion
  201.3 0.2 select_bitcast_fusion
  201.5 1.5 copy.9
  203.0 35.1 %all-reduce.2.cloned.1.call-done = f32[256,1024]{1,0:T(8,128)} async-done(((f32[256,1024]{1,0:T(8,128)}), f32[256,1024]{1,0:T(8,128)}) %all-reduce.2.cloned.1.call-update) | async-done | bytes 1048592 | tf_op jit(solution)/shard_map/psum | solution.py:28
  238.2 2.3 copy.26
  (18 shorter events, 0.1 us)
Async XLA Ops:
  8.0 1.6 copy-start
  8.0 191.0 %reduce-scatter.2.cloned.1.call-start = ((), (), s32[]{:S(2)}) async-start(), calls=%async_computation.2 | async-start | bytes 17825792 | tf_op jit(solution)/shard_map/reduce_scatter | solution.py:25
  18.8 180.3 %all-gather.2.cloned.1.call-start = ((), (), s32[]{:S(2)}) async-start(), calls=%async_computation.4 | async-start | bytes 3145728 | tf_op jit(solution)/shard_map/all_gather | solution.py:40
  22.2 176.8 %copy-start.1 = (s32[32]{0:T(128)S(1)}, s32[32]{0:T(128)}, u32[]{:S(2)}) copy-start(s32[32]{0:T(128)} %param.11) | copy-start | bytes 388
  54.2 183.9 %all-reduce.2.cloned.1.call-start = ((), (), s32[]{:S(2)}) async-start(), calls=%async_computation.3 | async-start | bytes 2097152 | tf_op jit(solution)/shard_map/psum | solution.py:28
Sparse Core Ops, SparseCore 0:
  18.9 180.0 reduce-scatter.1
Sparse Core Ops, SparseCore 1:
  54.3 33.3 all-gather.1
  199.1 39.0 all-reduce.1
